TPU v7x, 32 devices: a whole 2x2x4 slice. The times are simulated.
32 devices in a mesh: row: 8 (over z, x), col: 2 (over y), rep: 2 (over core).
Axes of the slice: x: 2, y: 2, z: 4, core: 2. Of those that a mesh axis runs over, the one named last changes fastest.
Arguments:
- matrix: float32 [16384, 16384], P('row', 'col'), may hold values from -0.125 to 0.125
- vectors: float32 [64, 16384], P('rep', 'row'), may hold values from -0.3 to 0.3
Outputs:
- result: float32 [64, 16384], P('rep', 'row')
All inputs are finite; a program needn't handle non-finite values.
Results may differ from a plain program's by a relative error of at most 0.00011.
Values sent between devices are 32-bit elements; how exact they have to be, the bound alone decides.
A program may use at most 128 MiB of HBM per device.

v0:
```python
import jax
import jax.numpy as jnp
from jax import lax
from jax.sharding import PartitionSpec as P

TERMS = 6
STEPS = 1


def broadcast(block, axis, holder):
    block = jnp.where(lax.axis_index(axis) == holder, block, jnp.zeros_like(block))
    return lax.psum(block, axis)


def apply_matrix(current, matrix):
    fanout = lax.axis_size("row") // lax.axis_size("col")
    column_index = lax.axis_index("col")
    pieces = [broadcast(current, "row", column_index * fanout + which) for which in range(fanout)]
    operand = jnp.concatenate(pieces, axis=1)
    partial_value = lax.dot_general(
        operand,
        matrix,
        (((1,), (1,)), ((), ())),
        precision=lax.Precision.HIGHEST,
        preferred_element_type=jnp.float32,
    )
    return lax.psum(partial_value, "col")


def local(matrix, vectors):
    summand = vectors
    running = vectors
    for degree in range(1, TERMS + 1):
        summand = apply_matrix(summand, matrix) / float(degree * STEPS)
        running = running + summand
    return running


def solution(mesh):
    placed = (P("row", "col"), P("rep", "row"))
    return jax.shard_map(
        local, mesh=mesh, in_specs=placed, out_specs=P("rep", "row"), check_vma=False
    )
```

profile of v0, /device:TPU:0, one launch (start us, length us, event | category | flops | bytes accessed | tf_op | source)
XLA Modules:
  0.0 1029.5 jit_solution(9411824174395434742)
XLA Ops:
  6.5 1.9 broadcast_select_fusion.7
  8.5 0.0 all-reduce.41.cloned.1.call-update
  8.5 0.0 all-reduce.19.cloned.1.call-start
  8.6 83.8 %all-reduce.41.cloned.1.call-done = (f32[32,2048]{1,0:T(8,128)}, f32[32,2048]{1,0:T(8,128)}, f32[32,2048]{1,0:T(8,128)}, f32[32,2048]{1,0:T(8,128)}) async-done(((f32[32,2048]{1,0:T(8,128)}, f32[32,2048]{1,0:T(8,128)}, f32[32,2048]{1,0:T(8,128)}, f32[32,2048]{1,0:T(8,128)}), (f32[32,2048]{1,0:T(8,128)}, f32[32,2048]{1,0:T(8,128)}, f32[32,2048]{1,0:T(8,128)}, ...) | async-done | bytes 1048592 | tf_op jit(solution)/shard_map/psum | solution.py:12
  92.4 63.2 %fusion = f32[32,2048]{1,0:T(8,128)} fusion(f32[2048,8192]{1,0:T(8,128)} %param.2, f32[32,2048]{1,0:T(8,128)} %get-tuple-element.25, f32[32,2048]{1,0:T(8,128)} %get-tuple-element.26, f32[32,2048]{1,0:T(8,128)} %get-tuple-element.27, f32[32,2048]{1,0:T(8,128)} %get-tuple-element.28), kind=kOutput, calls=%fused_computation | convolution fusion | flops 6443237376 | bytes 68419584 | tf_op jit(solution)/shard_map/dot_general | solution.py:20
  155.6 0.0 all-reduce.19.cloned.1.call-update
  155.6 0.0 all-reduce.39.cloned.1.call-start
  155.7 22.8 %all-reduce.19.cloned.1.call-done = f32[32,2048]{1,0:T(8,128)} async-done(((f32[32,2048]{1,0:T(8,128)}), f32[32,2048]{1,0:T(8,128)}) %all-reduce.19.cloned.1.call-update) | async-done | bytes 262160 | tf_op jit(solution)/shard_map/psum | solution.py:27
  178.5 1.9 broadcast_select_fusion.3
  180.4 0.0 all-reduce.39.cloned.1.call-update
  180.4 0.3 all-reduce.21.cloned.1.call-start
  180.8 80.1 %all-reduce.39.cloned.1.call-done = (f32[32,2048]{1,0:T(8,128)}, f32[32,2048]{1,0:T(8,128)}, f32[32,2048]{1,0:T(8,128)}, f32[32,2048]{1,0:T(8,128)}) async-done(((f32[32,2048]{1,0:T(8,128)}, f32[32,2048]{1,0:T(8,128)}, f32[32,2048]{1,0:T(8,128)}, f32[32,2048]{1,0:T(8,128)}), (f32[32,2048]{1,0:T(8,128)}, f32[32,2048]{1,0:T(8,128)}, f32[32,2048]{1,0:T(8,128)}, ...) | async-done | bytes 1048592 | tf_op jit(solution)/shard_map/psum | solution.py:12
  260.8 63.2 %fusion.8 = f32[32,2048]{1,0:T(8,128)} fusion(f32[2048,8192]{1,0:T(8,128)} %param.2, f32[32,2048]{1,0:T(8,128)} %get-tuple-element.21, f32[32,2048]{1,0:T(8,128)} %get-tuple-element.22, f32[32,2048]{1,0:T(8,128)} %get-tuple-element.23, f32[32,2048]{1,0:T(8,128)} %get-tuple-element.24), kind=kOutput, calls=%fused_computation.8 | convolution fusion | flops 6443237376 | bytes 68419584 | tf_op jit(solution)/shard_map/dot_general | solution.py:20
  324.1 0.0 all-reduce.21.cloned.1.call-update
  324.1 0.0 all-reduce.37.cloned.1.call-start
  324.1 22.8 %all-reduce.21.cloned.1.call-done = f32[32,2048]{1,0:T(8,128)} async-done(((f32[32,2048]{1,0:T(8,128)}), f32[32,2048]{1,0:T(8,128)}) %all-reduce.21.cloned.1.call-update) | async-done | bytes 262160 | tf_op jit(solution)/shard_map/psum | solution.py:27
  347.0 1.9 multiply_select_fusion.15
  348.9 0.0 all-reduce.37.cloned.1.call-update
  348.9 0.0 all-reduce.23.cloned.1.call-start
  349.0 80.1 %all-reduce.37.cloned.1.call-done = (f32[32,2048]{1,0:T(8,128)}, f32[32,2048]{1,0:T(8,128)}, f32[32,2048]{1,0:T(8,128)}, f32[32,2048]{1,0:T(8,128)}) async-done(((f32[32,2048]{1,0:T(8,128)}, f32[32,2048]{1,0:T(8,128)}, f32[32,2048]{1,0:T(8,128)}, f32[32,2048]{1,0:T(8,128)}), (f32[32,2048]{1,0:T(8,128)}, f32[32,2048]{1,0:T(8,128)}, f32[32,2048]{1,0:T(8,128)}, ...) | async-done | bytes 1048592 | tf_op jit(solution)/shard_map/psum | solution.py:12
  429.1 63.2 %fusion.16 = f32[32,2048]{1,0:T(8,128)} fusion(f32[2048,8192]{1,0:T(8,128)} %param.2, f32[32,2048]{1,0:T(8,128)} %get-tuple-element.17, f32[32,2048]{1,0:T(8,128)} %get-tuple-element.18, f32[32,2048]{1,0:T(8,128)} %get-tuple-element.19, f32[32,2048]{1,0:T(8,128)} %get-tuple-element.20), kind=kOutput, calls=%fused_computation.16 | convolution fusion | flops 6443237376 | bytes 68419584 | tf_op jit(solution)/shard_map/dot_general | solution.py:20
  492.3 0.0 all-reduce.23.cloned.1.call-update
  492.3 0.6 all-reduce.35.cloned.1.call-start
  492.9 22.3 %all-reduce.23.cloned.1.call-done = f32[32,2048]{1,0:T(8,128)} async-done(((f32[32,2048]{1,0:T(8,128)}), f32[32,2048]{1,0:T(8,128)}) %all-reduce.23.cloned.1.call-update) | async-done | bytes 262160 | tf_op jit(solution)/shard_map/psum | solution.py:27
  515.2 2.0 multiply_select_fusion.11
  517.1 0.0 all-reduce.35.cloned.1.call-update
  517.2 0.0 all-reduce.25.cloned.1.call-start
  517.2 80.3 %all-reduce.35.cloned.1.call-done = (f32[32,2048]{1,0:T(8,128)}, f32[32,2048]{1,0:T(8,128)}, f32[32,2048]{1,0:T(8,128)}, f32[32,2048]{1,0:T(8,128)}) async-done(((f32[32,2048]{1,0:T(8,128)}, f32[32,2048]{1,0:T(8,128)}, f32[32,2048]{1,0:T(8,128)}, f32[32,2048]{1,0:T(8,128)}), (f32[32,2048]{1,0:T(8,128)}, f32[32,2048]{1,0:T(8,128)}, f32[32,2048]{1,0:T(8,128)}, ...) | async-done | bytes 1048592 | tf_op jit(solution)/shard_map/psum | solution.py:12
  597.5 63.2 %fusion.24 = f32[32,2048]{1,0:T(8,128)} fusion(f32[2048,8192]{1,0:T(8,128)} %param.2, f32[32,2048]{1,0:T(8,128)} %get-tuple-element.13, f32[32,2048]{1,0:T(8,128)} %get-tuple-element.14, f32[32,2048]{1,0:T(8,128)} %get-tuple-element.15, f32[32,2048]{1,0:T(8,128)} %get-tuple-element.16), kind=kOutput, calls=%fused_computation.24 | convolution fusion | flops 6443237376 | bytes 68419584 | tf_op jit(solution)/shard_map/dot_general | solution.py:20
  660.7 0.0 all-reduce.25.cloned.1.call-update
  660.8 0.0 all-reduce.33.cloned.1.call-start
  660.8 22.8 %all-reduce.25.cloned.1.call-done = f32[32,2048]{1,0:T(8,128)} async-done(((f32[32,2048]{1,0:T(8,128)}), f32[32,2048]{1,0:T(8,128)}) %all-reduce.25.cloned.1.call-update) | async-done | bytes 262160 | tf_op jit(solution)/shard_map/psum | solution.py:27
  683.6 2.0 multiply_select_fusion.7
  685.6 0.0 all-reduce.33.cloned.1.call-update
  685.6 0.2 all-reduce.27.cloned.1.call-start
  685.8 80.2 %all-reduce.33.cloned.1.call-done = (f32[32,2048]{1,0:T(8,128)}, f32[32,2048]{1,0:T(8,128)}, f32[32,2048]{1,0:T(8,128)}, f32[32,2048]{1,0:T(8,128)}) async-done(((f32[32,2048]{1,0:T(8,128)}, f32[32,2048]{1,0:T(8,128)}, f32[32,2048]{1,0:T(8,128)}, f32[32,2048]{1,0:T(8,128)}), (f32[32,2048]{1,0:T(8,128)}, f32[32,2048]{1,0:T(8,128)}, f32[32,2048]{1,0:T(8,128)}, ...) | async-done | bytes 1048592 | tf_op jit(solution)/shard_map/psum | solution.py:12
  766.0 63.2 %fusion.32 = f32[32,2048]{1,0:T(8,128)} fusion(f32[2048,8192]{1,0:T(8,128)} %param.2, f32[32,2048]{1,0:T(8,128)} %get-tuple-element.9, f32[32,2048]{1,0:T(8,128)} %get-tuple-element.10, f32[32,2048]{1,0:T(8,128)} %get-tuple-element.11, f32[32,2048]{1,0:T(8,128)} %get-tuple-element.12), kind=kOutput, calls=%fused_computation.32 | convolution fusion | flops 6443237376 | bytes 68419584 | tf_op jit(solution)/shard_map/dot_general | solution.py:20
  829.3 0.0 all-reduce.27.cloned.1.call-update
  829.3 0.0 all-reduce.31.cloned.1.call-start
  829.3 22.8 %all-reduce.27.cloned.1.call-done = f32[32,2048]{1,0:T(8,128)} async-done(((f32[32,2048]{1,0:T(8,128)}), f32[32,2048]{1,0:T(8,128)}) %all-reduce.27.cloned.1.call-update) | async-done | bytes 262160 | tf_op jit(solution)/shard_map/psum | solution.py:27
  852.2 2.0 multiply_select_fusion.3
  854.2 0.0 all-reduce.31.cloned.1.call-update
  854.2 0.3 all-reduce.29.cloned.1.call-start
  854.5 80.1 %all-reduce.31.cloned.1.call-done = (f32[32,2048]{1,0:T(8,128)}, f32[32,2048]{1,0:T(8,128)}, f32[32,2048]{1,0:T(8,128)}, f32[32,2048]{1,0:T(8,128)}) async-done(((f32[32,2048]{1,0:T(8,128)}, f32[32,2048]{1,0:T(8,128)}, f32[32,2048]{1,0:T(8,128)}, f32[32,2048]{1,0:T(8,128)}), (f32[32,2048]{1,0:T(8,128)}, f32[32,2048]{1,0:T(8,128)}, f32[32,2048]{1,0:T(8,128)}, ...) | async-done | bytes 1048592 | tf_op jit(solution)/shard_map/psum | solution.py:12
  934.5 63.2 %fusion.40 = f32[32,2048]{1,0:T(8,128)} fusion(f32[2048,8192]{1,0:T(8,128)} %param.2, f32[32,2048]{1,0:T(8,128)} %get-tuple-element.5, f32[32,2048]{1,0:T(8,128)} %get-tuple-element.6, f32[32,2048]{1,0:T(8,128)} %get-tuple-element.7, f32[32,2048]{1,0:T(8,128)} %get-tuple-element.8), kind=kOutput, calls=%fused_computation.40 | convolution fusion | flops 6443237376 | bytes 68419584 | tf_op jit(solution)/shard_map/dot_general | solution.py:20
  997.8 0.0 all-reduce.29.cloned.1.call-update
  997.8 22.9 %all-reduce.29.cloned.1.call-done = f32[32,2048]{1,0:T(8,128)} async-done(((f32[32,2048]{1,0:T(8,128)}), f32[32,2048]{1,0:T(8,128)}) %all-reduce.29.cloned.1.call-update) | async-done | bytes 262160 | tf_op jit(solution)/shard_map/psum | solution.py:27
  1020.7 1.8 multiply_add_fusion
  (13 shorter events, 0.0 us)
Async XLA Ops:
  6.5 85.8 %all-reduce.41.cloned.1.call-start = ((), (), s32[]{:S(2)}) async-start(), calls=%async_computation.11 | async-start | bytes 2097152 | tf_op jit(solution)/shard_map/psum | solution.py:12
  8.5 170.0 %all-reduce.19.cloned.1.call-start = ((), (), s32[]{:S(2)}) async-start(), calls=%async_computation | async-start | bytes 524288 | tf_op jit(solution)/shard_map/psum | solution.py:27
  155.6 105.2 %all-reduce.39.cloned.1.call-start = ((), (), s32[]{:S(2)}) async-start(), calls=%async_computation.10 | async-start | bytes 2097152 | tf_op jit(solution)/shard_map/psum | solution.py:12
  180.4 166.5 %all-reduce.21.cloned.1.call-start = ((), (), s32[]{:S(2)}) async-start(), calls=%async_computation.1 | async-start | bytes 524288 | tf_op jit(solution)/shard_map/psum | solution.py:27
  324.1 105.0 %all-reduce.37.cloned.1.call-start = ((), (), s32[]{:S(2)}) async-start(), calls=%async_computation.9 | async-start | bytes 2097152 | tf_op jit(solution)/shard_map/psum | solution.py:12
  348.9 166.3 %all-reduce.23.cloned.1.call-start = ((), (), s32[]{:S(2)}) async-start(), calls=%async_computation.2 | async-start | bytes 524288 | tf_op jit(solution)/shard_map/psum | solution.py:27
  492.3 105.2 %all-reduce.35.cloned.1.call-start = ((), (), s32[]{:S(2)}) async-start(), calls=%async_computation.8 | async-start | bytes 2097152 | tf_op jit(solution)/shard_map/psum | solution.py:12
  517.2 166.5 %all-reduce.25.cloned.1.call-start = ((), (), s32[]{:S(2)}) async-start(), calls=%async_computation.3 | async-start | bytes 524288 | tf_op jit(solution)/shard_map/psum | solution.py:27
  660.8 105.2 %all-reduce.33.cloned.1.call-start = ((), (), s32[]{:S(2)}) async-start(), calls=%async_computation.7 | async-start | bytes 2097152 | tf_op jit(solution)/shard_map/psum | solution.py:12
  685.6 166.5 %all-reduce.27.cloned.1.call-start = ((), (), s32[]{:S(2)}) async-start(), calls=%async_computation.4 | async-start | bytes 524288 | tf_op jit(solution)/shard_map/psum | solution.py:27
  829.2 191.4 %copy-start = (f32[32,2048]{1,0:T(8,128)S(1)}, f32[32,2048]{1,0:T(8,128)}, u32[]{:S(2)}) copy-start(f32[32,2048]{1,0:T(8,128)} %param.3) | copy-start | bytes 786436
  829.2 191.4 %copy-start.1 = (f32[32,2048]{1,0:T(8,128)S(1)}, f32[32,2048]{1,0:T(8,128)}, u32[]{:S(2)}) copy-start(f32[32,2048]{1,0:T(8,128)} %all-reduce.19.cloned.1.call-done) | copy-start | bytes 786436
  829.2 191.4 %copy-start.2 = (f32[32,2048]{1,0:T(8,128)S(1)}, f32[32,2048]{1,0:T(8,128)}, u32[]{:S(2)}) copy-start(f32[32,2048]{1,0:T(8,128)} %all-reduce.21.cloned.1.call-done) | copy-start | bytes 786436
  829.2 191.4 %copy-start.3 = (f32[32,2048]{1,0:T(8,128)S(1)}, f32[32,2048]{1,0:T(8,128)}, u32[]{:S(2)}) copy-start(f32[32,2048]{1,0:T(8,128)} %all-reduce.23.cloned.1.call-done) | copy-start | bytes 786436
  829.2 191.4 %copy-start.4 = (f32[32,2048]{1,0:T(8,128)S(1)}, f32[32,2048]{1,0:T(8,128)}, u32[]{:S(2)}) copy-start(f32[32,2048]{1,0:T(8,128)} %all-reduce.25.cloned.1.call-done) | copy-start | bytes 786436
  829.3 105.2 %all-reduce.31.cloned.1.call-start = ((), (), s32[]{:S(2)}) async-start(), calls=%async_computation.6 | async-start | bytes 2097152 | tf_op jit(solution)/shard_map/psum | solution.py:12
  852.2 168.5 %copy-start.5 = (f32[32,2048]{1,0:T(8,128)S(1)}, f32[32,2048]{1,0:T(8,128)}, u32[]{:S(2)}) copy-start(f32[32,2048]{1,0:T(8,128)} %all-reduce.27.cloned.1.call-done) | copy-start | bytes 786436
  854.2 166.4 %all-reduce.29.cloned.1.call-start = ((), (), s32[]{:S(2)}) async-start(), calls=%async_computation.5 | async-start | bytes 524288 | tf_op jit(solution)/shard_map/psum | solution.py:27
Sparse Core Ops, SparseCore 0:
  11.2 81.1 all-reduce.40
  155.7 22.7 all-reduce.18
  182.3 78.4 all-reduce.38
  324.2 22.7 all-reduce.20
  350.7 78.3 all-reduce.36
  492.4 22.7 all-reduce.22
  519.0 78.4 all-reduce.34
  660.9 22.7 all-reduce.24
  687.5 78.4 all-reduce.32
  829.4 22.7 all-reduce.26
  856.0 78.4 all-reduce.30
  997.9 22.7 all-reduce.28
where the time goes:
time: 1030 us
  waiting for transfers between devices  621 us (60%)
  matrix products  379 us (37%)
  between operations  13.8 us (1%)
  other arithmetic  13.5 us (1%)
    psum x6, waiting for transfers between devices, broadcast(): return lax.psum(block, axis)  484 us
    dot_general x6, matrix products, apply_matrix(): lax.dot_general(operand, matrix, (((1,), (1,)), ((), ())), precision=lax....  379 us
    psum x6, waiting for transfers between devices, apply_matrix(): return lax.psum(partial_value, 'col')  136 us
  transfers between devices with their start and end apart: 12, of which 12 were waited for; matrix products, arithmetic and copies ran while one was open for 0% of the time, Pallas kernels for 0%

commit v1 on v0

v1 whole, which is shorter than its diff:
```python
import functools

import jax
import jax.numpy as jnp
from jax import lax
from jax.experimental import pallas as pl
from jax.experimental.pallas import tpu as pltpu
from jax.sharding import PartitionSpec as P

TERMS = 6
STEPS = 1
MESH = pl.DeviceIdType.MESH
TILE = 256
SLOTS = 4


def kernel(
    rows, cols, m_ref, v_ref, out_ref,
    high, low, stage, xbuf, acc, drecv, ybuf, run, fin, frecv,
    stage_sem, init_send, init_recv, x_recv, up_send, down_send, pair_send,
    d_send, d_recv, y_send, y_recv, f_send, f_recv,
):
    fanout = rows // cols
    size = m_ref.shape[0]
    share = v_ref.shape[0]
    half = size // 2
    chunks = half // TILE
    tiles = size // TILE
    lines = rows // 2
    depth = fanout // 2
    total = fanout * chunks

    r, c, p = lax.axis_index("row"), lax.axis_index("col"), lax.axis_index("rep")
    z, x = r // 2, r % 2
    first_line = c * depth
    owner = r // fanout
    own = owner == c
    mine = r % fanout

    barrier = pltpu.get_barrier_semaphore()

    def greet(**where):
        pl.semaphore_signal(barrier, inc=1, device_id=where, device_id_type=MESH)

    greet(rep=1 - p)
    greet(row=z * 2 + 1 - x)
    for offset in range(1, cols):
        greet(col=(c + offset) % cols)

    @pl.when(z > 0)
    def _():
        greet(row=r - 2)

    @pl.when(z < lines - 1)
    def _():
        greet(row=r + 2)

    def block_of(index):
        line = jnp.where(z > first_line, depth - 1 - index // 2, index // 2)
        lane = jnp.where(index % 2 == 0, x, 1 - x)
        return line, lane, line * 2 + lane

    def load(step):
        _, _, j = block_of(step % fanout)
        start = pl.multiple_of(j * size + p * half + (step // fanout) * TILE, TILE)
        return pltpu.make_async_copy(
            m_ref.at[:, pl.ds(start, TILE)], stage.at[step % SLOTS], stage_sem.at[step % SLOTS]
        )

    for step in range(min(SLOTS, total)):
        load(step).start()

    pl.semaphore_wait(barrier, 1 + cols + (z > 0).astype(jnp.int32) + (z < lines - 1).astype(jnp.int32))

    def remote(source, target, send, recv, **where):
        return pltpu.make_async_remote_copy(
            src_ref=source, dst_ref=target, send_sem=send, recv_sem=recv,
            device_id=where, device_id_type=MESH,
        )

    def hops(s, line, lane, j, k):
        ref, recv = xbuf.at[s, j, k], x_recv.at[s % 2, j, k]
        here = lane == x
        return (
            (here & (z >= line) & (z < lines - 1), remote(ref, ref, up_send.at[j, k], recv, row=r + 2)),
            (here & (z <= line) & (z > 0), remote(ref, ref, down_send.at[j, k], recv, row=r - 2)),
            (here, remote(ref, ref, pair_send.at[j, k], recv, row=z * 2 + 1 - x)),
        )

    def pass_on(s, line, lane, j, k, again):
        for needed, copy in hops(s, line, lane, j, k):
            @pl.when(needed)
            def _(copy=copy):
                if again:
                    copy.wait_send()
                copy.start()

    def pass_own(s, k, again):
        pass_on(s, z, x, mine, k, again)

    @pl.when(own)
    def _():
        def given(k):
            start = pl.multiple_of((1 - p) * half + k * TILE, TILE)
            return remote(
                v_ref.at[:, pl.ds(start, TILE)],
                xbuf.at[0, mine, k, pl.ds(pl.multiple_of(p * share, share), share), :],
                init_send.at[k], init_recv.at[k], rep=1 - p,
            )

        for k in range(chunks):
            given(k).start()
        for k in range(chunks):
            start = pl.multiple_of(p * half + k * TILE, TILE)
            xbuf[0, mine, k, pl.ds(pl.multiple_of(p * share, share), share), :] = v_ref[:, pl.ds(start, TILE)]
        for k in range(chunks):
            given(k).wait()
            run[k] = xbuf[0, mine, k]
            pass_own(0, k, False)

    @pl.when(jnp.logical_not(own))
    def _():
        run[...] = jnp.zeros_like(run)

    def prepare(step, index):
        load(step).wait()
        for n in range(tiles):
            block = stage[step % SLOTS, n * TILE:(n + 1) * TILE, :]
            top = block.astype(jnp.bfloat16)
            rest = (block - top.astype(jnp.float32)).astype(jnp.bfloat16)
            high[index, n] = top.T
            low[index, n] = rest.T

        @pl.when(step + SLOTS < total)
        def _():
            load(step + SLOTS).start()

    def multiply(s, first):
        acc[...] = jnp.zeros_like(acc)

        def body(step, carry):
            line, lane, j = block_of(step % fanout)
            k = step // fanout
            index = j * chunks + k
            if first:
                prepare(step, index)

            @pl.when(r != c * fanout + j)
            def _():
                remote(xbuf.at[s, j, k], xbuf.at[s, j, k], up_send.at[j, k], x_recv.at[s % 2, j, k], rep=1 - p).wait_recv()
                pass_on(s, first_line + line, lane, j, k, not first)

            value = xbuf[s, j, k]
            top = value.astype(jnp.bfloat16)
            rest = (value - top.astype(jnp.float32)).astype(jnp.bfloat16)
            both = jnp.concatenate([top, rest], axis=0)
            count = value.shape[0]
            for n in range(tiles):
                large = jnp.dot(both, high[index, n], preferred_element_type=jnp.float32)
                small = jnp.dot(top, low[index, n], preferred_element_type=jnp.float32)
                acc[n] += large[:count] + (large[count:] + small)
            return carry

        lax.fori_loop(0, total, body, 0)

    def swap(s, k):
        return remote(
            acc.at[(1 - p) * chunks + k], drecv.at[s, k], d_send.at[k], d_recv.at[s % 2, k], rep=1 - p
        )

    def to_column(s, k, target):
        return remote(
            ybuf.at[s, c, k], ybuf.at[s, c, k], y_send.at[target, k], y_recv.at[s % 2, c, k], col=target
        )

    def from_column(s, k, source):
        return remote(
            ybuf.at[s, source, k], ybuf.at[s, source, k], y_send.at[source, k], y_recv.at[s % 2, source, k], col=source
        )

    def column_sum(s, k):
        for offset in range(1, cols):
            from_column(s, k, (c + offset) % cols).wait_recv()
        value = ybuf[s, 0, k]
        for source in range(1, cols):
            value = value + ybuf[s, source, k]
        return value

    def scaled(s, k):
        swap(s, k).wait_recv()
        degree = jnp.asarray((s + 1) * STEPS, jnp.int32).astype(jnp.float32)
        return (acc[p * chunks + k] + drecv[s, k]) / degree

    def reduce(s, first):
        for k in range(chunks):
            swap(s, k).start()

        @pl.when(own)
        def _():
            for k in range(chunks):
                ybuf[s, c, k] = scaled(s, k)
                value = column_sum(s, k)
                xbuf[s + 1, mine, k] = value
                run[k] = run[k] + value
                pass_own(s + 1, k, True)

        @pl.when(jnp.logical_not(own))
        def _():
            for k in range(chunks):
                ybuf[s, c, k] = scaled(s, k)
                if not first:
                    to_column(s, k, owner).wait_send()
                to_column(s, k, owner).start()

        for k in range(chunks):
            swap(s, k).wait_send()

    multiply(0, True)
    reduce(0, True)

    def middle(s, carry):
        multiply(s, False)
        reduce(s, False)
        return carry

    lax.fori_loop(1, TERMS - 1, middle, 0)

    last = TERMS - 1
    multiply(last, False)
    for k in range(chunks):
        swap(last, k).start()
    for k in range(chunks):
        ybuf[last, c, k] = scaled(last, k) + run[k]

        @pl.when(jnp.logical_not(own))
        def _(k=k):
            to_column(last, k, owner).wait_send()

        for offset in range(1, cols):
            to_column(last, k, (c + offset) % cols).start()

    def give(k):
        part = pl.ds(pl.multiple_of((1 - p) * share, share), share)
        return remote(fin.at[k, part, :], frecv.at[k], f_send.at[k], f_recv.at[k], rep=1 - p)

    for k in range(chunks):
        fin[k] = column_sum(last, k)
        give(k).start()
        start = pl.multiple_of(p * half + k * TILE, TILE)
        out_ref[:, pl.ds(start, TILE)] = fin[k, pl.ds(pl.multiple_of(p * share, share), share), :]
    for k in range(chunks):
        give(k).wait()
        start = pl.multiple_of((1 - p) * half + k * TILE, TILE)
        out_ref[:, pl.ds(start, TILE)] = frecv[k]

    for k in range(chunks):
        swap(last, k).wait_send()
        for offset in range(1, cols):
            to_column(last, k, (c + offset) % cols).wait_send()

    def drain(step, carry):
        line, lane, j = block_of(step % fanout)
        for needed, copy in hops(last, first_line + line, lane, j, step // fanout):
            @pl.when(needed)
            def _(copy=copy):
                copy.wait_send()
        return carry

    lax.fori_loop(0, total, drain, 0)


def solution(mesh):
    rows, cols, reps = (mesh.shape[axis] for axis in ("row", "col", "rep"))

    def local(matrix, vectors):
        size, width = matrix.shape
        share = vectors.shape[0]
        every = share * reps
        fanout = rows // cols
        chunks = size // 2 // TILE
        tiles = size // TILE
        piece = (every, TILE)
        dma = pltpu.SemaphoreType.DMA
        return pl.pallas_call(
            functools.partial(kernel, rows, cols),
            out_shape=jax.ShapeDtypeStruct(vectors.shape, jnp.float32),
            in_specs=[pl.BlockSpec(memory_space=pltpu.HBM), pl.BlockSpec(memory_space=pltpu.VMEM)],
            out_specs=pl.BlockSpec(memory_space=pltpu.VMEM),
            scratch_shapes=[
                pltpu.VMEM((fanout * chunks, tiles, TILE, TILE), jnp.bfloat16),
                pltpu.VMEM((fanout * chunks, tiles, TILE, TILE), jnp.bfloat16),
                pltpu.VMEM((SLOTS, size, TILE), jnp.float32),
                pltpu.VMEM((TERMS, fanout, chunks) + piece, jnp.float32),
                pltpu.VMEM((tiles,) + piece, jnp.float32),
                pltpu.VMEM((TERMS, chunks) + piece, jnp.float32),
                pltpu.VMEM((TERMS, cols, chunks) + piece, jnp.float32),
                pltpu.VMEM((chunks,) + piece, jnp.float32),
                pltpu.VMEM((chunks,) + piece, jnp.float32),
                pltpu.VMEM((chunks, share, TILE), jnp.float32),
                dma((SLOTS,)),
                dma((chunks,)),
                dma((chunks,)),
                dma((2, fanout, chunks)),
                dma((fanout, chunks)),
                dma((fanout, chunks)),
                dma((fanout, chunks)),
                dma((chunks,)),
                dma((2, chunks)),
                dma((cols, chunks)),
                dma((2, cols, chunks)),
                dma((chunks,)),
                dma((chunks,)),
            ],
            compiler_params=pltpu.CompilerParams(
                collective_id=0, has_side_effects=True, vmem_limit_bytes=63 * 1024 * 1024
            ),
        )(matrix, vectors)

    return jax.shard_map(
        local, mesh=mesh, in_specs=(P("row", "col"), P("rep", "row")), out_specs=P("rep", "row"), check_vma=False
    )
```

time: 1030 us -> 267 us (0.26)
  waiting for transfers between devices: 621 us -> 0 us
  matrix products: 379 us -> 0 us
  Pallas kernels: 0 us -> 265 us
  between operations: 13.8 us -> 0.01 us
  other arithmetic: 13.5 us -> 0 us
    psum x12 -> x0, waiting for transfers between devices: 621 us -> none  [the longest x6 484 us: broadcast(): return lax.psum(block, axis)]
    dot_general x6 -> x0, matrix products: 379 us -> none  [apply_matrix(): lax.dot_general(operand, matrix, (((1,), (1,)), ((), ())), precision=lax....]
    pallas_call x0 -> x1, Pallas kernels: none -> 265 us  [local(): pl.pallas_call(functools.partial(kernel, rows, cols), out_shape=jax.Shape...]
    select_n x6 -> x0, other arithmetic: 11.8 us -> none  [broadcast(): jnp.where(lax.axis_index(axis) == holder, block, jnp.zeros_like(block))]
  transfers between devices with their start and end apart: 12 -> 0, of which waited for: 12 -> 0; matrix products, arithmetic and copies ran while one was open for 0% -> 0% of each run, Pallas kernels for 0% -> 0%
where the time goes in v1:
time: 267 us
  Pallas kernels  265 us (99%)
    pallas_call x1, Pallas kernels, local(): pl.pallas_call(functools.partial(kernel, rows, cols), out_shape=jax.Shape...  265 us

profile of v1, /device:TPU:0, one launch (start us, length us, event | category | flops | bytes accessed | tf_op | source)
XLA Modules:
  0.0 267.1 jit_solution(8289764174933584861)
XLA Ops:
  0.0 265.4 %shard_map.28 = f32[32,2048]{1,0:T(8,128)} custom-call(f32[2048,8192]{1,0:T(8,128)} %m_ref.1, f32[32,2048]{1,0:T(8,128)} %v_ref.1), custom_call_target="tpu_custom_call" | custom-call | tf_op jit(solution)/shard_map/pallas_call | solution.py:284
  265.4 1.7 copy.4

commit v2 on v1

--- a/solution.py
+++ b/solution.py
@@ -12,6 +12,7 @@
 MESH = pl.DeviceIdType.MESH
 TILE = 256
 SLOTS = 4
+LAG = 4
 
 
 def kernel(
@@ -55,14 +56,21 @@
     def _():
         greet(row=r + 2)
 
-    def block_of(index):
-        line = jnp.where(z > first_line, depth - 1 - index // 2, index // 2)
-        lane = jnp.where(index % 2 == 0, x, 1 - x)
-        return line, lane, line * 2 + lane
+    def chunk_of(step):
+        count = total // 2
+        lag = min(LAG, count)
+        mixed = step - lag
+        alternate = jnp.where(mixed % 2 == 0, count + mixed // 2, lag + mixed // 2)
+        place = jnp.where(step < lag, step, jnp.where(step < 2 * count - lag, alternate, step))
+        other, place = place // count, place % count
+        near = place // chunks
+        line = jnp.where(z > first_line, depth - 1 - near, near)
+        lane = jnp.where(other == 0, x, 1 - x)
+        return line, lane, line * 2 + lane, place % chunks
 
     def load(step):
-        _, _, j = block_of(step % fanout)
-        start = pl.multiple_of(j * size + p * half + (step // fanout) * TILE, TILE)
+        _, _, j, k = chunk_of(step)
+        start = pl.multiple_of(j * size + p * half + k * TILE, TILE)
         return pltpu.make_async_copy(
             m_ref.at[:, pl.ds(start, TILE)], stage.at[step % SLOTS], stage_sem.at[step % SLOTS]
         )
@@ -139,8 +147,7 @@
         acc[...] = jnp.zeros_like(acc)
 
         def body(step, carry):
-            line, lane, j = block_of(step % fanout)
-            k = step // fanout
+            line, lane, j, k = chunk_of(step)
             index = j * chunks + k
             if first:
                 prepare(step, index)
@@ -259,8 +266,8 @@
             to_column(last, k, (c + offset) % cols).wait_send()
 
     def drain(step, carry):
-        line, lane, j = block_of(step % fanout)
-        for needed, copy in hops(last, first_line + line, lane, j, step // fanout):
+        line, lane, j, k = chunk_of(step)
+        for needed, copy in hops(last, first_line + line, lane, j, k):
             @pl.when(needed)
             def _(copy=copy):
                 copy.wait_send()

time: 267 us -> 160 us (0.60)
  Pallas kernels: 265 us -> 158 us
    pallas_call x1, Pallas kernels: 265 us -> 158 us  [local(): pl.pallas_call(functools.partial(kernel, rows, cols), out_shape=jax.Shape...]
where the time goes in v2:
time: 160 us; the launch traced here: 159 us
  Pallas kernels  158 us (99%)
  local copies, waits for them, and re-layouts  1.67 us (1%)
    pallas_call x1, Pallas kernels, local(): pl.pallas_call(functools.partial(kernel, rows, cols), out_shape=jax.Shape...  158 us

profile of v2, /device:TPU:0, one launch (start us, length us, event | category | flops | bytes accessed | tf_op | source)
XLA Modules:
  0.0 159.4 jit_solution(8430099671867082963)
XLA Ops:
  0.0 157.7 %shard_map.28 = f32[32,2048]{1,0:T(8,128)} custom-call(f32[2048,8192]{1,0:T(8,128)} %m_ref.1, f32[32,2048]{1,0:T(8,128)} %v_ref.1), custom_call_target="tpu_custom_call" | custom-call | tf_op jit(solution)/shard_map/pallas_call | solution.py:291
  157.7 1.7 %copy.4 = f32[32,2048]{1,0:T(8,128)} copy(f32[32,2048]{1,0:T(8,128)} %shard_map.28) | data formatting | bytes 524288

commit v3 on v2

--- a/solution.py
+++ b/solution.py
@@ -12,7 +12,8 @@
 MESH = pl.DeviceIdType.MESH
 TILE = 256
 SLOTS = 4
-LAG = 4
+LAG = 5
+SPLIT = 2
 
 
 def kernel(
@@ -86,25 +87,27 @@
             device_id=where, device_id_type=MESH,
         )
 
-    def hops(s, line, lane, j, k):
-        ref, recv = xbuf.at[s, j, k], x_recv.at[s % 2, j, k]
+    part = share * 2 // SPLIT
+
+    def hops(s, line, lane, j, k, h):
+        ref, recv = xbuf.at[s, j, k, pl.ds(h * part, part), :], x_recv.at[s % 2, j, k, h]
         here = lane == x
         return (
-            (here & (z >= line) & (z < lines - 1), remote(ref, ref, up_send.at[j, k], recv, row=r + 2)),
-            (here & (z <= line) & (z > 0), remote(ref, ref, down_send.at[j, k], recv, row=r - 2)),
-            (here, remote(ref, ref, pair_send.at[j, k], recv, row=z * 2 + 1 - x)),
+            (here & (z >= line) & (z < lines - 1), remote(ref, ref, up_send.at[j, k, h], recv, row=r + 2)),
+            (here & (z <= line) & (z > 0), remote(ref, ref, down_send.at[j, k, h], recv, row=r - 2)),
+            (here, remote(ref, ref, pair_send.at[j, k, h], recv, row=z * 2 + 1 - x)),
         )
 
-    def pass_on(s, line, lane, j, k, again):
-        for needed, copy in hops(s, line, lane, j, k):
+    def pass_on(s, line, lane, j, k, h, again):
+        for needed, copy in hops(s, line, lane, j, k, h):
             @pl.when(needed)
             def _(copy=copy):
                 if again:
                     copy.wait_send()
                 copy.start()
 
-    def pass_own(s, k, again):
-        pass_on(s, z, x, mine, k, again)
+    def pass_own(s, k, h, again):
+        pass_on(s, z, x, mine, k, h, again)
 
     @pl.when(own)
     def _():
@@ -124,7 +127,8 @@
         for k in range(chunks):
             given(k).wait()
             run[k] = xbuf[0, mine, k]
-            pass_own(0, k, False)
+            for h in range(SPLIT):
+                pass_own(0, k, h, False)
 
     @pl.when(jnp.logical_not(own))
     def _():
@@ -154,8 +158,10 @@
 
             @pl.when(r != c * fanout + j)
             def _():
-                remote(xbuf.at[s, j, k], xbuf.at[s, j, k], up_send.at[j, k], x_recv.at[s % 2, j, k], rep=1 - p).wait_recv()
-                pass_on(s, first_line + line, lane, j, k, not first)
+                for h in range(SPLIT):
+                    ref = xbuf.at[s, j, k, pl.ds(h * part, part), :]
+                    remote(ref, ref, up_send.at[j, k, h], x_recv.at[s % 2, j, k, h], rep=1 - p).wait_recv()
+                    pass_on(s, first_line + line, lane, j, k, h, not first)
 
             value = xbuf[s, j, k]
             top = value.astype(jnp.bfloat16)
@@ -175,22 +181,20 @@
             acc.at[(1 - p) * chunks + k], drecv.at[s, k], d_send.at[k], d_recv.at[s % 2, k], rep=1 - p
         )
 
-    def to_column(s, k, target):
-        return remote(
-            ybuf.at[s, c, k], ybuf.at[s, c, k], y_send.at[target, k], y_recv.at[s % 2, c, k], col=target
-        )
-
-    def from_column(s, k, source):
-        return remote(
-            ybuf.at[s, source, k], ybuf.at[s, source, k], y_send.at[source, k], y_recv.at[s % 2, source, k], col=source
-        )
-
-    def column_sum(s, k):
+    def to_column(s, k, h, target):
+        ref = ybuf.at[s, c, k, pl.ds(h * part, part), :]
+        return remote(ref, ref, y_send.at[target, k, h], y_recv.at[s % 2, c, k, h], col=target)
+
+    def from_column(s, k, h, source):
+        ref = ybuf.at[s, source, k, pl.ds(h * part, part), :]
+        return remote(ref, ref, y_send.at[source, k, h], y_recv.at[s % 2, source, k, h], col=source)
+
+    def column_sum(s, k, h):
         for offset in range(1, cols):
-            from_column(s, k, (c + offset) % cols).wait_recv()
-        value = ybuf[s, 0, k]
+            from_column(s, k, h, (c + offset) % cols).wait_recv()
+        value = ybuf[s, 0, k, h * part:(h + 1) * part, :]
         for source in range(1, cols):
-            value = value + ybuf[s, source, k]
+            value = value + ybuf[s, source, k, h * part:(h + 1) * part, :]
         return value
 
     def scaled(s, k):
@@ -206,18 +210,21 @@
         def _():
             for k in range(chunks):
                 ybuf[s, c, k] = scaled(s, k)
-                value = column_sum(s, k)
-                xbuf[s + 1, mine, k] = value
-                run[k] = run[k] + value
-                pass_own(s + 1, k, True)
+                for h in range(SPLIT):
+                    piece = slice(h * part, (h + 1) * part)
+                    value = column_sum(s, k, h)
+                    xbuf[s + 1, mine, k, piece, :] = value
+                    run[k, piece, :] = run[k, piece, :] + value
+                    pass_own(s + 1, k, h, True)
 
         @pl.when(jnp.logical_not(own))
         def _():
             for k in range(chunks):
                 ybuf[s, c, k] = scaled(s, k)
-                if not first:
-                    to_column(s, k, owner).wait_send()
-                to_column(s, k, owner).start()
+                for h in range(SPLIT):
+                    if not first:
+                        to_column(s, k, h, owner).wait_send()
+                    to_column(s, k, h, owner).start()
 
         for k in range(chunks):
             swap(s, k).wait_send()
@@ -241,17 +248,20 @@
 
         @pl.when(jnp.logical_not(own))
         def _(k=k):
-            to_column(last, k, owner).wait_send()
+            for h in range(SPLIT):
+                to_column(last, k, h, owner).wait_send()
 
         for offset in range(1, cols):
-            to_column(last, k, (c + offset) % cols).start()
+            for h in range(SPLIT):
+                to_column(last, k, h, (c + offset) % cols).start()
 
     def give(k):
-        part = pl.ds(pl.multiple_of((1 - p) * share, share), share)
-        return remote(fin.at[k, part, :], frecv.at[k], f_send.at[k], f_recv.at[k], rep=1 - p)
-
-    for k in range(chunks):
-        fin[k] = column_sum(last, k)
+        theirs = pl.ds(pl.multiple_of((1 - p) * share, share), share)
+        return remote(fin.at[k, theirs, :], frecv.at[k], f_send.at[k], f_recv.at[k], rep=1 - p)
+
+    for k in range(chunks):
+        for h in range(SPLIT):
+            fin[k, h * part:(h + 1) * part, :] = column_sum(last, k, h)
         give(k).start()
         start = pl.multiple_of(p * half + k * TILE, TILE)
         out_ref[:, pl.ds(start, TILE)] = fin[k, pl.ds(pl.multiple_of(p * share, share), share), :]
@@ -263,14 +273,16 @@
     for k in range(chunks):
         swap(last, k).wait_send()
         for offset in range(1, cols):
-            to_column(last, k, (c + offset) % cols).wait_send()
+            for h in range(SPLIT):
+                to_column(last, k, h, (c + offset) % cols).wait_send()
 
     def drain(step, carry):
         line, lane, j, k = chunk_of(step)
-        for needed, copy in hops(last, first_line + line, lane, j, k):
-            @pl.when(needed)
-            def _(copy=copy):
-                copy.wait_send()
+        for h in range(SPLIT):
+            for needed, copy in hops(last, first_line + line, lane, j, k, h):
+                @pl.when(needed)
+                def _(copy=copy):
+                    copy.wait_send()
         return carry
 
     lax.fori_loop(0, total, drain, 0)
@@ -307,14 +319,14 @@
                 dma((SLOTS,)),
                 dma((chunks,)),
                 dma((chunks,)),
-                dma((2, fanout, chunks)),
-                dma((fanout, chunks)),
-                dma((fanout, chunks)),
-                dma((fanout, chunks)),
+                dma((2, fanout, chunks, SPLIT)),
+                dma((fanout, chunks, SPLIT)),
+                dma((fanout, chunks, SPLIT)),
+                dma((fanout, chunks, SPLIT)),
                 dma((chunks,)),
                 dma((2, chunks)),
-                dma((cols, chunks)),
-                dma((2, cols, chunks)),
+                dma((cols, chunks, SPLIT)),
+                dma((2, cols, chunks, SPLIT)),
                 dma((chunks,)),
                 dma((chunks,)),
             ],

time: 160 us -> 155 us (0.969)
  Pallas kernels: 158 us -> 153 us
    pallas_call x1, Pallas kernels: 158 us -> 153 us  [local(): pl.pallas_call(functools.partial(kernel, rows, cols), out_shape=jax.Shape...]
where the time goes in v3:
time: 155 us
  Pallas kernels  153 us (99%)
  local copies, waits for them, and re-layouts  1.67 us (1%)
    pallas_call x1, Pallas kernels, local(): pl.pallas_call(functools.partial(kernel, rows, cols), out_shape=jax.Shape...  153 us

profile of v3, /device:TPU:0, one launch (start us, length us, event | category | flops | bytes accessed | tf_op | source)
XLA Modules:
  0.0 154.7 jit_solution(16738812355299390917)
XLA Ops:
  0.0 153.0 %shard_map.28 = f32[32,2048]{1,0:T(8,128)} custom-call(f32[2048,8192]{1,0:T(8,128)} %m_ref.1, f32[32,2048]{1,0:T(8,128)} %v_ref.1), custom_call_target="tpu_custom_call" | custom-call | tf_op jit(solution)/shard_map/pallas_call | solution.py:303
  153.0 1.7 %copy.4 = f32[32,2048]{1,0:T(8,128)} copy(f32[32,2048]{1,0:T(8,128)} %shard_map.28) | data formatting | bytes 524288
